TPU v7x, 128 devices: a whole 4x4x4 slice. The times are simulated.
128 devices in a mesh: head: 8 (over y, core), row: 16 (over x, z).
Axes of the slice: x: 4, y: 4, z: 4, core: 2. Of those that a mesh axis runs over, the one named last changes fastest.
Arguments:
- hidden_in: bfloat16 [512, 2048], replicated, may hold values from -6 to 6
- w_query: bfloat16 [2048, 16, 128], P(None, 'head', 'row'), may hold values from -0.125 to 0.125
- w_key: bfloat16 [2048, 16, 128], P(None, 'head', 'row'), may hold values from -0.125 to 0.125
- w_value: bfloat16 [2048, 32, 128], P(None, 'head'), may hold values from -0.125 to 0.125
- w_zgate: bfloat16 [2048, 32, 128], P(None, 'head'), may hold values from -0.125 to 0.125
- w_decay: bfloat16 [2048, 32], P(None, 'head'), may hold values from -0.125 to 0.125
- w_beta: bfloat16 [2048, 32], P(None, 'head'), may hold values from -0.125 to 0.125
- decay_log: float32 [32], P('head'), may hold values from -1.5 to 1.5
- dt_bias: float32 [32], P('head'), may hold values from -2 to 2
- norm_gain: float32 [128], replicated, may hold values from 0.1 to 1.9
- w_out: bfloat16 [32, 128, 2048], P('head'), may hold values from -0.09375 to 0.09375
- state: float32 [512, 32, 128, 128], P(None, 'head', 'row'), may hold values from -6 to 6
Outputs:
- layer_out: bfloat16 [512, 2048], P('row', 'head')
- new_state: float32 [512, 32, 128, 128], P(None, 'head', 'row')
All inputs are finite; a program needn't handle non-finite values.
Results may differ from a plain program's by a relative error of at most 0.005.
Values sent between devices are 32-bit elements; how exact they have to be, the bound alone decides.
No kernel may reach another device: no remote copies, remote signals or barrier semaphores. Data moves between devices by JAX's collectives and lax.ppermute only.
A program may use at most 128 MiB of HBM per device.

v0:
```python
import jax
import jax.numpy as jnp
from jax import lax
from jax.experimental import pallas as pl
from jax.experimental.pallas import tpu as pltpu
from jax.sharding import PartitionSpec as P


LANES = 128
SUB = 8
BLOCK = 16
SIDE = 4
KEY_HEADS = 2


def high_low(value):
    high = value.astype(jnp.bfloat16)
    return high, (value - high.astype(jnp.float32)).astype(jnp.bfloat16)


def dot(left, right):
    return jnp.dot(left, right, preferred_element_type=jnp.float32)


def read_kernel(
    hidden_hbm,
    w_query_hbm,
    w_key_hbm,
    w_decay_hbm,
    w_beta_hbm,
    decay_log_hbm,
    dt_bias_hbm,
    state_hbm,
    *rest,
):
    by_x, by_z = rest[0:SIDE], rest[SIDE : 2 * SIDE]
    keys_hbm, decay_hbm, decay_own, beta_own = rest[2 * SIDE : 2 * SIDE + 4]
    hidden, weights, w_decay, w_beta, decay_log, dt_bias, state = rest[2 * SIDE + 4 : 2 * SIDE + 11]
    reads_k, left, picks, sums, keys_all, decay_all, beta_all = rest[2 * SIDE + 11 : 2 * SIDE + 18]
    in_sems, hidden_sems, state_sems, k_sems, out_sems = rest[2 * SIDE + 18 :]
    me = lax.axis_index("row")
    my_x, my_z = me // SIDE, me % SIDE
    _, rows, heads = state.shape[0:3]
    chunks = hidden.shape[0]
    blocks = LANES // BLOCK
    key_rows = w_query_hbm.shape[0]
    key_heads = key_rows // SUB
    group = heads // key_heads
    few = BLOCK
    span = few * SUB
    pad = weights.dtype.itemsize * SUB

    inputs = [
        pltpu.make_async_copy(w_query_hbm, weights.at[pad : pad + key_rows], in_sems.at[0]),
        pltpu.make_async_copy(w_key_hbm, weights.at[pad + key_rows : pad + 2 * key_rows], in_sems.at[1]),
        pltpu.make_async_copy(w_decay_hbm, w_decay, in_sems.at[2]),
        pltpu.make_async_copy(decay_log_hbm, decay_log, in_sems.at[3]),
        pltpu.make_async_copy(dt_bias_hbm, dt_bias, in_sems.at[4]),
        pltpu.make_async_copy(w_beta_hbm, w_beta, in_sems.at[5]),
    ]
    for copy in inputs:
        copy.start()

    def chunk_of(s):
        return (my_x + s) % SIDE

    def hidden_copy(s):
        at = pl.multiple_of(chunk_of(s) * LANES, LANES)
        return pltpu.make_async_copy(hidden_hbm.at[pl.ds(at, LANES)], hidden.at[s], hidden_sems.at[s])

    def state_copy(n):
        part = chunk_of(n // SIDE) * SIDE + (my_z + n % SIDE) % SIDE
        return pltpu.make_async_copy(state_hbm.at[pl.ds(part * rows, rows)], state.at[n], state_sems.at[n])

    def k_copy(s, to):
        return pltpu.make_async_copy(reads_k.at[s], to, k_sems.at[s])

    ahead = 2
    for n in range(ahead):
        hidden_copy(n).start()
    width = weights.shape[1]
    weights[0:pad] = jnp.zeros((pad, width), weights.dtype)
    weights[pad + 2 * key_rows :] = jnp.zeros((LANES - pad - 2 * key_rows, width), weights.dtype)
    sums[...] = jnp.zeros(sums.shape, sums.dtype)
    source = lax.broadcasted_iota(jnp.int32, (LANES, span), 0)
    entry = lax.broadcasted_iota(jnp.int32, (LANES, span), 1) % SUB
    own = lax.broadcasted_iota(jnp.int32, (few, span), 1) // SUB == lax.broadcasted_iota(jnp.int32, (few, span), 0)
    for n in range(2 * key_heads):
        picks[n] = (source == pad + n * SUB + entry).astype(jnp.bfloat16)
    for copy in inputs:
        copy.wait()
    weights[0:heads] = w_decay[...]
    weights[heads : 2 * heads] = w_beta[...]
    for n in range(ahead * SIDE):
        state_copy(n).start()
        if n % SIDE == 1:
            hidden_copy(ahead + n // SIDE).start()

    @pl.loop(0, chunks)
    def _(s):
        chunk = chunk_of(s)
        hidden_copy(s).wait()

        @pl.when(s + ahead < SIDE)
        def _():
            for t in range(SIDE):
                state_copy((s + ahead) * SIDE + t).start()

        projected = lax.dot_general(hidden[s], weights[...], (((1,), (1,)), ((), ())), preferred_element_type=jnp.float32)
        halves = jnp.concatenate(high_low(projected), axis=0)
        for n in range(2 * key_heads):
            wide = dot(halves, picks[n]).reshape(2 * blocks, few, span)
            left[n] = jnp.where(own[None], wide, 0.0).astype(jnp.bfloat16)

        at = pl.multiple_of(chunk * LANES, LANES)
        pre = projected[:, 0:heads] + dt_bias[...]
        soft = jnp.maximum(pre, 0.0) + jnp.log1p(jnp.exp(-jnp.abs(pre)))
        decay_all[pl.ds(at, LANES)] = jnp.exp(-jnp.exp(decay_log[...]) * soft)
        beta_all[pl.ds(at, LANES)] = 1.0 / (1.0 + jnp.exp(-projected[:, heads : 2 * heads]))
        turned = jnp.transpose(projected)
        query = turned[pad : pad + key_rows]
        keys = turned[pad + key_rows : pad + 2 * key_rows]
        keys_all[:, pl.ds(at, LANES)] = keys
        for n, product in enumerate((query * query, keys * keys, query * keys)):
            for g in range(key_heads):
                sums[n * key_heads + g : n * key_heads + g + 1] = jnp.sum(product[g * SUB : (g + 1) * SUB], axis=0, keepdims=True)

        for t in range(SIDE):
            p = (my_z + t) % SIDE
            turn = s * SIDE + t
            state_copy(turn).wait()
            for first in range(0, rows, few):
                block = p * (rows // few) + first // few
                for g in range(key_heads):
                    tiles = [state[turn, first : first + few, g * group + j].reshape(span, LANES) for j in range(group)]
                    state_high, state_low = high_low(jnp.concatenate(tiles, axis=1))
                    high = jnp.concatenate([left[g, block], left[key_heads + g, block]], axis=0)
                    low = jnp.concatenate([left[g, blocks + block], left[key_heads + g, blocks + block]], axis=0)
                    both = dot(jnp.concatenate([high, low], axis=0), state_high)
                    read = both[0 : 2 * few] + both[2 * few :] + dot(high, state_low)
                    for j in range(group):
                        to = (g * group + j) * rows + first
                        lanes = slice(j * LANES, (j + 1) * LANES)
                        reads_k[s, t, to : to + few] = read[few:, lanes]
                        by_z[t][s, to : to + few] = read[0:few, lanes]
            reads_k[s, t, heads * rows :] = pltpu.roll(sums[...], (LANES - p * rows) % LANES, 1)
        for k in range(SIDE):

            @pl.when(s == k)
            def _():
                k_copy(s, by_x[k]).start()

    outputs = [
        pltpu.make_async_copy(keys_all, keys_hbm, out_sems.at[0]),
        pltpu.make_async_copy(decay_all, decay_hbm, out_sems.at[1]),
    ]
    for copy in outputs:
        copy.start()

    mine = pl.ds(pl.multiple_of(me * rows, rows), rows)
    decay_own[...] = decay_all[mine]
    beta_own[...] = beta_all[mine]
    for k in range(SIDE):
        k_copy(k, by_x[k]).wait()
    for copy in outputs:
        copy.wait()


def arrived_sum(parts):
    return (parts[0][...] + parts[1][...]) + (parts[2][...] + parts[3][...])


def delta_kernel(*refs):
    values, decay, beta, delta_hbm, delta_out, scaled, out_sems = refs[SIDE:]
    rows, heads = decay.shape
    parts = delta_hbm.shape[0]
    read_k = arrived_sum(refs[0:SIDE])
    raw_sums = read_k[heads * rows :]
    delta_out[heads * rows :] = raw_sums
    sums = jnp.transpose(raw_sums)[0:rows]
    group = heads // KEY_HEADS
    key_scale = lax.rsqrt(1.0 + sums[:, KEY_HEADS : 2 * KEY_HEADS])
    for h in range(heads):
        g = h // group
        at = slice(h * rows, (h + 1) * rows)
        ks = key_scale[:, g : g + 1]
        readk = read_k[at] * ks
        delta = beta[:, h : h + 1] * (values[h] - decay[:, h : h + 1] * readk)
        delta_out[at] = delta
        scaled[at] = delta * ks
    outputs = [pltpu.make_async_copy(scaled, delta_hbm.at[n], out_sems.at[n]) for n in range(parts)]
    for copy in outputs:
        copy.start()
    for copy in outputs:
        copy.wait()


def norm_kernel(*refs):
    deltas, zgate, decay, norm_gain, normed_out = refs[SIDE:]
    rows, heads = decay.shape
    read_q = arrived_sum(refs[0:SIDE])
    sums = jnp.transpose(deltas[heads * rows :])[0:rows]
    group = heads // KEY_HEADS
    query_scale = lax.rsqrt(1.0 + sums[:, 0:KEY_HEADS])
    key_scale = lax.rsqrt(1.0 + sums[:, KEY_HEADS : 2 * KEY_HEADS])
    unit_dot = sums[:, 2 * KEY_HEADS : 3 * KEY_HEADS] * query_scale * key_scale
    for h in range(heads):
        g = h // group
        lanes = slice(h * LANES, (h + 1) * LANES)
        at = slice(h * rows, (h + 1) * rows)
        readq = decay[:, h : h + 1] * (read_q[at] * query_scale[:, g : g + 1]) + unit_dot[:, g : g + 1] * deltas[at]
        meansq = jnp.mean(readq * readq, axis=1, keepdims=True)
        z = zgate[h]
        normed = readq * lax.rsqrt(meansq + 0.5) * norm_gain[...] * (z / (1.0 + jnp.exp(-z)))
        normed_out[:, lanes] = normed.astype(jnp.bfloat16)


def update_kernel(delta, keys_hbm, decay_hbm, state_hbm, new_state, keys, decay, wide, state, ready, small_sems, in_sems, out_sems):
    parts, rows, heads = state.shape[0:3]
    key_heads = keys.shape[0] // SUB
    group = heads // key_heads
    few = BLOCK
    span = few * SUB
    per_tile = LANES // rows

    small = [
        pltpu.make_async_copy(decay_hbm, decay, small_sems.at[0]),
        pltpu.make_async_copy(keys_hbm, keys, small_sems.at[1]),
    ]
    for copy in small:
        copy.start()

    def read(n):
        return pltpu.make_async_copy(state_hbm.at[pl.ds(n * rows, rows)], state.at[n], in_sems.at[n])

    def write(n):
        return pltpu.make_async_copy(ready.at[n], new_state.at[pl.ds(n * rows, rows)], out_sems.at[n])

    ahead = 6
    for n in range(ahead):
        read(n).start()
    lane = lax.broadcasted_iota(jnp.int32, (SUB, LANES), 1)
    slot = lax.broadcasted_iota(jnp.int32, (span, LANES), 1)
    own = (slot % few == lax.broadcasted_iota(jnp.int32, (span, LANES), 0) // SUB) & (slot < 3 * few)
    ones = jnp.ones((LANES, LANES), jnp.bfloat16)
    for copy in small:
        copy.wait()

    @pl.loop(0, parts // per_tile)
    def _(n):
        at = pl.multiple_of(n * LANES, LANES)
        some = decay[pl.ds(at, LANES)]
        for h in range(heads):
            spread = jnp.broadcast_to(some[:, h : h + 1], (LANES, LANES)).reshape(per_tile, rows, LANES)
            wide[pl.ds(n * per_tile, per_tile), :, h * LANES : (h + 1) * LANES] = spread

    @pl.loop(0, parts // per_tile)
    def _(tile):
        raw = keys[:, pl.ds(pl.multiple_of(tile * LANES, LANES), LANES)]
        high = raw.astype(jnp.bfloat16).astype(jnp.float32)
        rest = raw - high
        middle = rest.astype(jnp.bfloat16).astype(jnp.float32)
        low = rest - middle
        for n in range(per_tile):
            part = tile * per_tile + n
            read(part).wait()

            @pl.when(part + ahead < parts)
            def _():
                read(part + ahead).start()

            for first in range(0, rows, few):
                back = LANES - n * rows - first
                turned = [pltpu.roll(x, (back + m * few) % LANES, 1) for m, x in enumerate((high, middle, low))]
                packed = jnp.where(lane[0:1] < few, turned[0], jnp.where(lane[0:1] < 2 * few, turned[1], turned[2]))
                for g in range(key_heads):
                    spread = jnp.broadcast_to(packed[None, g * SUB : (g + 1) * SUB], (few, SUB, LANES)).reshape(span, LANES)
                    wide_key = dot(jnp.where(own, spread, 0.0).astype(jnp.bfloat16), ones)
                    for b in range(few):
                        k = wide_key[b * SUB : (b + 1) * SUB]
                        at = first + b
                        for h in range(g * group, (g + 1) * group):
                            row = jnp.broadcast_to(delta[part, h * rows + at : h * rows + at + 1], (SUB, LANES))
                            factor = jnp.broadcast_to(wide[part, at : at + 1, h * LANES : (h + 1) * LANES], (SUB, LANES))
                            ready[part, at, h] = factor * state[part, at, h] + k * row
            write(part).start()

    @pl.loop(0, parts)
    def _(part):
        write(part).wait()


def project_kernel(core, normed, w_out_hbm, give, keep, w_out, sem):
    copy = pltpu.make_async_copy(w_out_hbm, w_out, sem)
    copy.start()
    copy.wait()
    total = dot(normed[...], w_out[...])
    size = give.shape[2]
    first = core[0] == 0
    for y in range(give.shape[0]):
        even = total[:, 2 * y * size : (2 * y + 1) * size]
        odd = total[:, (2 * y + 1) * size : (2 * y + 2) * size]
        keep[y] = jnp.where(first, even, odd)
        give[y] = jnp.where(first, odd, even)


def chip_kernel(y, keep, got, own, *away):
    size = keep.shape[0]
    own[...] = keep[y[0]] + got[y[0]]
    for n, out in enumerate(away):
        at = (y[0] + n + 1) % size
        out[...] = keep[at] + got[at]


def head_exchange(normed, w_out, y_size):
    rows = normed.shape[0]
    heads = 2 * y_size
    size = w_out.shape[1] // heads
    head = lax.axis_index("head")
    in_smem = pl.BlockSpec(memory_space=pltpu.SMEM)
    in_vmem = pl.BlockSpec(memory_space=pltpu.VMEM)
    limit = pltpu.CompilerParams(vmem_limit_bytes=8 * 1024 * 1024)
    piece = jax.ShapeDtypeStruct((y_size, rows, size), jnp.float32)
    give, keep = pl.pallas_call(
        project_kernel,
        in_specs=[in_smem, in_vmem, pl.BlockSpec(memory_space=pl.ANY)],
        out_specs=[in_vmem, in_vmem],
        out_shape=[piece, piece],
        scratch_shapes=[pltpu.VMEM(w_out.shape, w_out.dtype), pltpu.SemaphoreType.DMA],
        compiler_params=limit,
        name="project_out",
    )((head % 2)[None], normed, pltpu.with_memory_space_constraint(w_out, pltpu.HBM))
    got = lax.ppermute(give, "head", [(h, h ^ 1) for h in range(heads)])
    total, *away = pl.pallas_call(
        chip_kernel,
        in_specs=[in_smem, in_vmem, in_vmem],
        out_specs=[in_vmem] * y_size,
        out_shape=[jax.ShapeDtypeStruct((rows, size), jnp.float32)] * y_size,
        compiler_params=limit,
        name="chip_sum",
    )((head // 2)[None], keep, got)
    for s, part in enumerate(away, 1):
        total = total + lax.ppermute(part, "head", [(h, (h + 2 * s) % heads) for h in range(heads)])
    return total


def decode(
    hidden_in,
    w_query,
    w_key,
    w_value,
    w_zgate,
    w_decay,
    w_beta,
    decay_log,
    dt_bias,
    norm_gain,
    w_out,
    state,
):
    parts = lax.axis_size("row")
    seqs, width = hidden_in.shape
    rows = seqs // parts
    heads = state.shape[1]
    key_rows = w_query.shape[1] * w_query.shape[2]
    f32 = jnp.float32

    def in_hbm(value):
        return pltpu.with_memory_space_constraint(value, pltpu.HBM)

    any_space = pl.BlockSpec(memory_space=pl.ANY)
    in_vmem = pl.BlockSpec(memory_space=pltpu.VMEM)
    limit = pltpu.CompilerParams(vmem_limit_bytes=20 * 1024 * 1024)
    extra = heads * rows + SUB
    per_k, per_q = (SIDE, extra, LANES), (SIDE, heads * rows, LANES)
    *sent, keys, decay_all, decay, beta = pl.pallas_call(
        read_kernel,
        in_specs=[any_space] * 8,
        out_specs=[in_vmem] * (2 * SIDE) + [any_space] * 2 + [in_vmem] * 2,
        out_shape=[pltpu.VMEM(per_k, f32)] * SIDE
        + [pltpu.VMEM(per_q, f32)] * SIDE
        + [pltpu.HBM((key_rows, seqs), f32), pltpu.HBM((seqs, heads), f32)]
        + [jax.ShapeDtypeStruct((rows, heads), f32)] * 2,
        scratch_shapes=[
            pltpu.VMEM((seqs // LANES, LANES, width), jnp.bfloat16),
            pltpu.VMEM((LANES, width), jnp.bfloat16),
            pltpu.VMEM((heads, width), jnp.bfloat16),
            pltpu.VMEM((heads, width), jnp.bfloat16),
            pltpu.VMEM((1, heads), f32),
            pltpu.VMEM((1, heads), f32),
            pltpu.VMEM((parts, rows, heads, SUB, LANES), f32),
            pltpu.VMEM((SIDE, *per_k), f32),
            pltpu.VMEM((2 * key_rows // SUB, 2 * LANES // BLOCK, BLOCK, BLOCK * SUB), jnp.bfloat16),
            pltpu.VMEM((2 * key_rows // SUB, LANES, BLOCK * SUB), jnp.bfloat16),
            pltpu.VMEM((SUB, LANES), f32),
            pltpu.VMEM((key_rows, seqs), f32),
            pltpu.VMEM((seqs, heads), f32),
            pltpu.VMEM((seqs, heads), f32),
            pltpu.SemaphoreType.DMA((6,)),
            pltpu.SemaphoreType.DMA((seqs // LANES,)),
            pltpu.SemaphoreType.DMA((parts,)),
            pltpu.SemaphoreType.DMA((SIDE,)),
            pltpu.SemaphoreType.DMA((2,)),
        ],
        compiler_params=limit,
        name="read_state",
    )(
        in_hbm(hidden_in),
        in_hbm(jnp.transpose(w_query, (1, 2, 0)).reshape(key_rows, width)),
        in_hbm(jnp.transpose(w_key, (1, 2, 0)).reshape(key_rows, width)),
        in_hbm(jnp.transpose(w_decay)),
        in_hbm(jnp.transpose(w_beta)),
        in_hbm(decay_log[None]),
        in_hbm(dt_bias[None]),
        in_hbm(state),
    )

    def along_x(value, step):
        return lax.ppermute(value, "row", [(n, (n + SIDE * step) % parts) for n in range(parts)])

    def along_z(value, step):
        return lax.ppermute(value, "row", [(n, n // SIDE * SIDE + (n + step) % SIDE) for n in range(parts)])

    steps = (1, 3, 2)
    pairs = [(along_x(sent[n], n), along_z(sent[SIDE + n], n)) for n in steps]
    got_k, got_q = zip(*pairs)
    part_k, part_q = (
        [(own[n] + got[0][n]) + (got[1][n] + got[2][n]) for n in range(SIDE)]
        for own, got in ((sent[0], got_k), (sent[SIDE], got_q))
    )
    arrived_k = [part_k[0], *(along_z(part_k[n], n) for n in steps)]
    arrived_q = [part_q[0], *(along_x(part_q[n], n) for n in steps)]

    own_hidden = lax.dynamic_slice_in_dim(hidden_in, lax.axis_index("row") * rows, rows, 0)
    values = jnp.einsum("bd,dhv->hbv", own_hidden, w_value, preferred_element_type=f32)
    zgate = jnp.einsum("bd,dhv->hbv", own_hidden, w_zgate, preferred_element_type=f32)

    delta_sent, delta_own = pl.pallas_call(
        delta_kernel,
        in_specs=[in_vmem] * (SIDE + 3),
        out_specs=[any_space, in_vmem],
        out_shape=[
            pltpu.HBM((parts, heads * rows, LANES), f32),
            jax.ShapeDtypeStruct((extra, LANES), f32),
        ],
        scratch_shapes=[
            pltpu.VMEM((heads * rows, LANES), f32),
            pltpu.SemaphoreType.DMA((parts,)),
        ],
        compiler_params=limit,
        name="owner_delta",
    )(*arrived_k, values, decay, beta)
    delta = lax.all_to_all(delta_sent, "row", 0, 0, tiled=True)

    normed = pl.pallas_call(
        norm_kernel,
        in_specs=[in_vmem] * (SIDE + 4),
        out_specs=in_vmem,
        out_shape=jax.ShapeDtypeStruct((rows, heads * LANES), jnp.bfloat16),
        compiler_params=limit,
        name="owner_norm",
    )(*arrived_q, delta_own, zgate, decay, norm_gain[None])

    layer_out = head_exchange(normed, w_out.reshape(heads * LANES, -1), lax.axis_size("head") // 2).astype(jnp.bfloat16)

    new_state = pl.pallas_call(
        update_kernel,
        in_specs=[in_vmem, any_space, any_space, any_space],
        out_specs=any_space,
        out_shape=pltpu.HBM(state.shape, f32),
        scratch_shapes=[
            pltpu.VMEM((key_rows, seqs), f32),
            pltpu.VMEM((seqs, heads), f32),
            pltpu.VMEM((parts, rows, heads * LANES), f32),
            pltpu.VMEM((parts, rows, heads, SUB, LANES), f32),
            pltpu.VMEM((parts, rows, heads, SUB, LANES), f32),
            pltpu.SemaphoreType.DMA((2,)),
            pltpu.SemaphoreType.DMA((parts,)),
            pltpu.SemaphoreType.DMA((parts,)),
        ],
        compiler_params=pltpu.CompilerParams(vmem_limit_bytes=24 * 1024 * 1024),
        name="update_state",
    )(delta, in_hbm(keys), in_hbm(decay_all), in_hbm(state))
    return (layer_out, new_state)


def solution(mesh):
    in_specs = (
        P(),
        P(None, "head", "row"),
        P(None, "head", "row"),
        P(None, "head", None),
        P(None, "head", None),
        P(None, "head"),
        P(None, "head"),
        P("head"),
        P("head"),
        P(),
        P("head", None, None),
        P(None, "head", "row", None),
    )
    out_specs = (P("row", "head"), P(None, "head", "row", None))
    return jax.shard_map(decode, mesh=mesh, in_specs=in_specs, out_specs=out_specs, check_vma=False)
```

profile of v0, /device:TPU:0, one launch (start us, length us, event | category | flops | bytes accessed | tf_op | source)
XLA Modules:
  0.0 90.8 jit_solution(12279256639495173061)
XLA Ops:
  0.6 0.0 copy-start
  0.6 10.1 %read_state.1 = (f32[4,136,128]{2,1,0:T(8,128)S(1)}, f32[4,136,128]{2,1,0:T(8,128)S(1)}, f32[4,136,128]{2,1,0:T(8,128)S(1)}, f32[4,136,128]{2,1,0:T(8,128)S(1)},...) custom-call(bf16[512,2048]{1,0:T(8,128)(2,1)} %hidden_hbm.1, ...), custom_call_target="tpu_custom_call" | custom-call | tf_op jit(solution)/shard_map/read_state/pallas_call | solution.py:376
  10.7 0.0 copy-start.1
  10.7 1.7 %collective-permute-start.6 = (f32[4,136,128]{2,1,0:T(8,128)S(1)}, f32[4,136,128]{2,1,0:T(8,128)S(1)}, u32[]{:S(2)}, u32[]{:S(2)}) collective-permute-start(f32[4,136,128]{2,1,0:T(8,128)S(1)} %get-tuple-element.27), channel_id=1, source_target_pairs={{0,4},{1,5},{2,6},{3,7},{4,8},{5,9},{6,10},{7,11},{8,12},{9,13},{1... | collective-permute-start | bytes 835592 | tf_op jit(solution)/shard_map/ppermute | solution.py:419
  12.4 1.6 %collective-permute-start.7 = (f32[4,136,128]{2,1,0:T(8,128)S(1)}, f32[4,136,128]{2,1,0:T(8,128)S(1)}, u32[]{:S(2)}, u32[]{:S(2)}) collective-permute-start(f32[4,136,128]{2,1,0:T(8,128)S(1)} %get-tuple-element.28), channel_id=1, source_target_pairs={{0,12},{1,13},{2,14},{3,15},{4,0},{5,1},{6,2},{7,3},{8,4},{9,5},{1... | collective-permute-start | bytes 835592 | tf_op jit(solution)/shard_map/ppermute | solution.py:419
  14.0 1.9 %collective-permute-start.8 = (f32[4,136,128]{2,1,0:T(8,128)S(1)}, f32[4,136,128]{2,1,0:T(8,128)S(1)}, u32[]{:S(2)}, u32[]{:S(2)}) collective-permute-start(f32[4,136,128]{2,1,0:T(8,128)S(1)} %get-tuple-element.29), channel_id=1, source_target_pairs={{0,8},{1,9},{2,10},{3,11},{4,12},{5,13},{6,14},{7,15},{8,0},{9,1},... | collective-permute-start | bytes 835592 | tf_op jit(solution)/shard_map/ppermute | solution.py:419
  16.0 4.4 %collective-permute-done.6 = f32[4,136,128]{2,1,0:T(8,128)S(1)} collective-permute-done((f32[4,136,128]{2,1,0:T(8,128)S(1)}, f32[4,136,128]{2,1,0:T(8,128)S(1)}, u32[]{:S(2)}, u32[]{:S(2)}) %collective-permute-start.6) | collective-permute-done | bytes 278560 | tf_op jit(solution)/shard_map/ppermute | solution.py:419
  20.3 1.6 %collective-permute-done.7 = f32[4,136,128]{2,1,0:T(8,128)S(1)} collective-permute-done((f32[4,136,128]{2,1,0:T(8,128)S(1)}, f32[4,136,128]{2,1,0:T(8,128)S(1)}, u32[]{:S(2)}, u32[]{:S(2)}) %collective-permute-start.7) | collective-permute-done | bytes 278560 | tf_op jit(solution)/shard_map/ppermute | solution.py:419
  21.9 5.5 %collective-permute-done.8 = f32[4,136,128]{2,1,0:T(8,128)S(1)} collective-permute-done((f32[4,136,128]{2,1,0:T(8,128)S(1)}, f32[4,136,128]{2,1,0:T(8,128)S(1)}, u32[]{:S(2)}, u32[]{:S(2)}) %collective-permute-start.8) | collective-permute-done | bytes 278560 | tf_op jit(solution)/shard_map/ppermute | solution.py:419
  27.5 0.1 fusion.15
  27.5 4.0 %collective-permute-start.11 = (f32[136,128]{1,0:T(8,128)S(1)}, f32[136,128]{1,0:T(8,128)S(1)}, u32[]{:S(2)}, u32[]{:S(2)}) collective-permute-start(f32[136,128]{1,0:T(8,128)S(1)} %get-tuple-element.42), channel_id=1, source_target_pairs={{0,2},{1,3},{2,0},{3,1},{4,6},{5,7},{6,4},{7,5},{8,10},{9,11},{10,... | collective-permute-start | bytes 208904 | tf_op jit(solution)/shard_map/ppermute | solution.py:422
  31.5 1.0 %collective-permute-start = (f32[4,128,128]{2,1,0:T(8,128)}, f32[4,128,128]{2,1,0:T(8,128)}, u32[]{:S(2)}, u32[]{:S(2)}) collective-permute-start(f32[4,128,128]{2,1,0:T(8,128)} %get-tuple-element.23), channel_id=1, source_target_pairs={{0,1},{1,2},{2,3},{3,0},{4,5},{5,6},{6,7},{7,4},{8,9},{9,10},{10,1... | collective-permute-start | bytes 786440 | tf_op jit(solution)/shard_map/ppermute | solution.py:422
  32.5 2.2 %collective-permute-start.1 = (f32[4,128,128]{2,1,0:T(8,128)}, f32[4,128,128]{2,1,0:T(8,128)}, u32[]{:S(2)}, u32[]{:S(2)}) collective-permute-start(f32[4,128,128]{2,1,0:T(8,128)} %get-tuple-element.24), channel_id=1, source_target_pairs={{0,3},{1,0},{2,1},{3,2},{4,7},{5,4},{6,5},{7,6},{8,11},{9,8},{10,9... | collective-permute-start | bytes 786440 | tf_op jit(solution)/shard_map/ppermute | solution.py:422
  34.7 0.0 collective-permute-start.2
  34.7 2.5 %collective-permute-start.10 = (f32[136,128]{1,0:T(8,128)S(1)}, f32[136,128]{1,0:T(8,128)S(1)}, u32[]{:S(2)}, u32[]{:S(2)}) collective-permute-start(f32[136,128]{1,0:T(8,128)S(1)} %get-tuple-element.43), channel_id=1, source_target_pairs={{0,3},{1,0},{2,1},{3,2},{4,7},{5,4},{6,5},{7,6},{8,11},{9,8},{10,9... | collective-permute-start | bytes 208904 | tf_op jit(solution)/shard_map/ppermute | solution.py:422
  37.2 0.0 collective-permute-done.11.refs_3_
  37.2 0.0 collective-permute-start.9
  37.2 0.0 copy-done
  37.2 1.4 %fusion.4.refs_4_ = f32[4,32,128]{2,1,0:T(8,128)S(1)} fusion(bf16[2048,4,128]{2,1,0:T(4,128)(2,1)S(1)} %copy-done, bf16[512,2048]{1,0:T(8,128)(2,1)} %hidden_hbm.1, s32[]{:T(128)S(6)} %select_n.16), kind=kOutput, calls=%fused_computation.4 | convolution fusion | flops 67108864 | bytes 2293764 | tf_op jit(solution)/shard_map/bd,dhv->hbv/dot_general | solution.py:435
  38.6 8.7 %collective-permute-done.10.refs_2_ = f32[136,128]{1,0:T(8,128)S(1)} collective-permute-done((f32[136,128]{1,0:T(8,128)S(1)}, f32[136,128]{1,0:T(8,128)S(1)}, u32[]{:S(2)}, u32[]{:S(2)}) %collective-permute-start.10) | collective-permute-done | bytes 69664 | tf_op jit(solution)/shard_map/ppermute | solution.py:422
  47.2 0.0 collective-permute-done.9.refs_1_
  47.2 1.3 %owner_delta.1 = (f32[16,128,128]{2,1,0:T(8,128)}, f32[136,128]{1,0:T(8,128)S(1)}) custom-call(f32[136,128]{1,0:T(8,128)S(1)} %get-tuple-element.45.refs_0_, f32[136,128]{1,0:T(8,128)S(1)} %collective-permute-done.9.refs_1_, f32[136,128]{1,0:T(8,128)S(1)} %collective-permute-done.10.refs_2_, f32[136,128]{1,0:T(8,128)S(1)} %collective-permute-done.11.refs_3_, ...), custom_call_target="tpu_custom_call" | custom-call | tf_op jit(solution)/shard_map/owner_delta/pallas_call | solution.py:438
  48.5 0.0 copy-done.1
  48.5 5.7 %all-to-all-start = ((f32[16,128,128]{2,1,0:T(8,128)}), f32[16,128,128]{2,1,0:T(8,128)S(1)}, u32[]{:S(2)}, u32[]{:S(2)}) async-start(f32[16,128,128]{2,1,0:T(8,128)} %get-tuple-element.39), calls=%async_computation | async-start | bytes 2097152 | tf_op jit(solution)/shard_map/all_to_all | solution.py:453
  54.2 0.0 copy-start.4
  54.2 0.0 collective-permute-done
  54.2 0.0 collective-permute-done.1
  54.2 0.0 collective-permute-done.2
  54.3 1.9 %fusion.23 = (f32[128,128]{1,0:T(8,128)}, f32[128,128]{1,0:T(8,128)}, f32[128,128]{1,0:T(8,128)}, f32[128,128]{1,0:T(8,128)S(1)}) fusion(f32[4,128,128]{2,1,0:T(8,128)} %collective-permute-done.2, f32[4,128,128]{2,1,0:T(8,128)} %collective-permute-done.1, f32[4,128,128]{2,1,0:T(8,128)} %collective-permute-done, f32[4,128,128]{2,1,0:T(8,128)S(1)} %get-tuple-element.22), kind=kLoop, calls=%fused_computation.28 | loop fusion | flops 196608 | bytes 1310720 | tf_op jit(solution)/shard_map/add | solution.py:428
  56.1 0.0 copy-start.2
  56.1 3.4 %collective-permute-start.5 = (f32[128,128]{1,0:T(8,128)}, f32[128,128]{1,0:T(8,128)S(1)}, u32[]{:S(2)}, u32[]{:S(2)}) collective-permute-start(f32[128,128]{1,0:T(8,128)} %get-tuple-element.46), channel_id=1, source_target_pairs={{0,8},{1,9},{2,10},{3,11},{4,12},{5,13},{6,14},{7,15},{8,0},{9,1},... | collective-permute-start | bytes 196616 | tf_op jit(solution)/shard_map/ppermute | solution.py:419
  59.6 1.2 %collective-permute-start.4 = (f32[128,128]{1,0:T(8,128)}, f32[128,128]{1,0:T(8,128)S(1)}, u32[]{:S(2)}, u32[]{:S(2)}) collective-permute-start(f32[128,128]{1,0:T(8,128)} %get-tuple-element.47), channel_id=1, source_target_pairs={{0,12},{1,13},{2,14},{3,15},{4,0},{5,1},{6,2},{7,3},{8,4},{9,5},{1... | collective-permute-start | bytes 196616 | tf_op jit(solution)/shard_map/ppermute | solution.py:419
  60.7 0.9 collective-permute-start.3
  61.6 2.8 %fusion.7.refs_5_ = f32[4,32,128]{2,1,0:T(8,128)} fusion(bf16[2048,4,128]{2,1,0:T(4,128)(2,1)} %param.16, bf16[512,2048]{1,0:T(8,128)(2,1)} %hidden_hbm.1, s32[]{:T(128)S(6)} %select_n.16), kind=kOutput, calls=%fused_computation.5 | convolution fusion | flops 67108864 | bytes 2293764 | tf_op jit(solution)/shard_map/bd,dhv->hbv/dot_general | solution.py:436
  64.3 4.0 %collective-permute-done.5.refs_3_ = f32[128,128]{1,0:T(8,128)S(1)} collective-permute-done((f32[128,128]{1,0:T(8,128)}, f32[128,128]{1,0:T(8,128)S(1)}, u32[]{:S(2)}, u32[]{:S(2)}) %collective-permute-start.5) | collective-permute-done | bytes 65568 | tf_op jit(solution)/shard_map/ppermute | solution.py:419
  68.4 0.0 collective-permute-done.4.refs_2_
  68.4 0.6 collective-permute-done.3.refs_1_
  68.9 0.0 copy-done.4
  68.9 0.0 copy-done.2
  68.9 0.0 copy-start.3
  68.9 0.8 copy-done.3
  69.8 0.3 owner_norm.1.normed
  70.1 2.1 %project_out.1 = (f32[4,32,256]{2,1,0:T(8,128)S(1)}, f32[4,32,256]{2,1,0:T(8,128)S(1)}) custom-call(s32[1]{0:T(128)} %bitcast.1.core, bf16[32,512]{1,0:T(8,128)(2,1)S(1)} %owner_norm.1.normed, bf16[512,2048]{1,0:T(8,128)(2,1)} %bitcast.40), custom_call_target="tpu_custom_call" | custom-call | tf_op jit(solution)/shard_map/project_out/pallas_call | solution.py:324
  72.2 0.1 collective-permute-start.12
  72.3 1.3 %collective-permute-done.12.got = f32[4,32,256]{2,1,0:T(8,128)S(1)} collective-permute-done((f32[4,32,256]{2,1,0:T(8,128)S(1)}, f32[4,32,256]{2,1,0:T(8,128)S(1)}, u32[]{:S(2)}, u32[]{:S(2)}) %collective-permute-start.12) | collective-permute-done | bytes 131104 | tf_op jit(solution)/shard_map/ppermute | solution.py:333
  73.6 1.6 %collective-permute-start.13 = (f32[32,256]{1,0:T(8,128)S(1)}, f32[32,256]{1,0:T(8,128)S(1)}, u32[]{:S(2)}, u32[]{:S(2)}) collective-permute-start(f32[32,256]{1,0:T(8,128)S(1)} %get-tuple-element.36), channel_id=1, source_target_pairs={{0,32},{16,48},{32,64},{48,80},{64,96},{80,112},{96,0},{112,16},{1... | collective-permute-start | bytes 98312 | tf_op jit(solution)/shard_map/ppermute | solution.py:343
  75.3 2.9 %collective-permute-start.14 = (f32[32,256]{1,0:T(8,128)S(1)}, f32[32,256]{1,0:T(8,128)S(1)}, u32[]{:S(2)}, u32[]{:S(2)}) collective-permute-start(f32[32,256]{1,0:T(8,128)S(1)} %get-tuple-element.37), channel_id=1, source_target_pairs={{0,64},{16,80},{32,96},{48,112},{64,0},{80,16},{96,32},{112,48},{1... | collective-permute-start | bytes 98312 | tf_op jit(solution)/shard_map/ppermute | solution.py:343
  78.2 1.3 %collective-permute-start.15 = (f32[32,256]{1,0:T(8,128)S(1)}, f32[32,256]{1,0:T(8,128)S(1)}, u32[]{:S(2)}, u32[]{:S(2)}) collective-permute-start(f32[32,256]{1,0:T(8,128)S(1)} %get-tuple-element.38), channel_id=1, source_target_pairs={{0,96},{16,112},{32,0},{48,16},{64,32},{80,48},{96,64},{112,80},{1... | collective-permute-start | bytes 98312 | tf_op jit(solution)/shard_map/ppermute | solution.py:343
  79.5 0.0 collective-permute-done.13
  79.5 1.2 %collective-permute-done.14 = f32[32,256]{1,0:T(8,128)S(1)} collective-permute-done((f32[32,256]{1,0:T(8,128)S(1)}, f32[32,256]{1,0:T(8,128)S(1)}, u32[]{:S(2)}, u32[]{:S(2)}) %collective-permute-start.14) | collective-permute-done | bytes 32800 | tf_op jit(solution)/shard_map/ppermute | solution.py:343
  80.7 1.4 %collective-permute-done.15 = f32[32,256]{1,0:T(8,128)S(1)} collective-permute-done((f32[32,256]{1,0:T(8,128)S(1)}, f32[32,256]{1,0:T(8,128)S(1)}, u32[]{:S(2)}, u32[]{:S(2)}) %collective-permute-start.15) | collective-permute-done | bytes 32800 | tf_op jit(solution)/shard_map/ppermute | solution.py:343
  82.1 0.6 add_convert_fusion
  82.7 0.0 all-to-all-done.delta
  82.7 8.1 %update_state.1 = f32[512,4,8,128]{3,2,1,0:T(8,128)} custom-call(f32[16,128,128]{2,1,0:T(8,128)S(1)} %all-to-all-done.delta, f32[16,512]{1,0:T(8,128)} %get-tuple-element.40.keys_hbm, f32[512,4]{1,0:T(8,128)} %get-tuple-element.41.decay_hbm, f32[512,4,8,128]{3,2,1,0:T(8,128)} %state_hbm.3), custom_call_target="tpu_custom_call" | custom-call | tf_op jit(solution)/shard_map/update_state/pallas_call | solution.py:466
  (1 shorter events, 0.0 us)
Async XLA Ops:
  0.6 36.6 %copy-start = (bf16[2048,4,128]{2,1,0:T(4,128)(2,1)S(1)}, bf16[2048,4,128]{2,1,0:T(4,128)(2,1)}, u32[]{:S(2)}) copy-start(bf16[2048,4,128]{2,1,0:T(4,128)(2,1)} %param.15) | copy-start | bytes 6291460
  10.7 37.8 %copy-start.1 = (f32[32,4]{1,0:T(8,128)}, f32[32,4]{1,0:T(8,128)S(1)}, u32[]{:S(2)}) copy-start(f32[32,4]{1,0:T(8,128)S(1)} %get-tuple-element.30.refs_5_.refs_6_) | copy-start | bytes 1540
  10.7 9.6 %collective-permute-start.6 = (f32[4,136,128]{2,1,0:T(8,128)S(1)}, f32[4,136,128]{2,1,0:T(8,128)S(1)}, u32[]{:S(2)}, u32[]{:S(2)}) collective-permute-start(f32[4,136,128]{2,1,0:T(8,128)S(1)} %get-tuple-element.27), channel_id=1, source_target_pairs={{0,4},{1,5},{2,6},{3,7},{4,8},{5,9},{6,10},{7,11},{8,12},{9,13},{1... | collective-permute-start | bytes 835592 | tf_op jit(solution)/shard_map/ppermute | solution.py:419
  12.4 9.5 %collective-permute-start.7 = (f32[4,136,128]{2,1,0:T(8,128)S(1)}, f32[4,136,128]{2,1,0:T(8,128)S(1)}, u32[]{:S(2)}, u32[]{:S(2)}) collective-permute-start(f32[4,136,128]{2,1,0:T(8,128)S(1)} %get-tuple-element.28), channel_id=1, source_target_pairs={{0,12},{1,13},{2,14},{3,15},{4,0},{5,1},{6,2},{7,3},{8,4},{9,5},{1... | collective-permute-start | bytes 835592 | tf_op jit(solution)/shard_map/ppermute | solution.py:419
  14.0 13.4 %collective-permute-start.8 = (f32[4,136,128]{2,1,0:T(8,128)S(1)}, f32[4,136,128]{2,1,0:T(8,128)S(1)}, u32[]{:S(2)}, u32[]{:S(2)}) collective-permute-start(f32[4,136,128]{2,1,0:T(8,128)S(1)} %get-tuple-element.29), channel_id=1, source_target_pairs={{0,8},{1,9},{2,10},{3,11},{4,12},{5,13},{6,14},{7,15},{8,0},{9,1},... | collective-permute-start | bytes 835592 | tf_op jit(solution)/shard_map/ppermute | solution.py:419
  27.5 9.7 %collective-permute-start.11 = (f32[136,128]{1,0:T(8,128)S(1)}, f32[136,128]{1,0:T(8,128)S(1)}, u32[]{:S(2)}, u32[]{:S(2)}) collective-permute-start(f32[136,128]{1,0:T(8,128)S(1)} %get-tuple-element.42), channel_id=1, source_target_pairs={{0,2},{1,3},{2,0},{3,1},{4,6},{5,7},{6,4},{7,5},{8,10},{9,11},{10,... | collective-permute-start | bytes 208904 | tf_op jit(solution)/shard_map/ppermute | solution.py:422
  31.5 22.7 %collective-permute-start = (f32[4,128,128]{2,1,0:T(8,128)}, f32[4,128,128]{2,1,0:T(8,128)}, u32[]{:S(2)}, u32[]{:S(2)}) collective-permute-start(f32[4,128,128]{2,1,0:T(8,128)} %get-tuple-element.23), channel_id=1, source_target_pairs={{0,1},{1,2},{2,3},{3,0},{4,5},{5,6},{6,7},{7,4},{8,9},{9,10},{10,1... | collective-permute-start | bytes 786440 | tf_op jit(solution)/shard_map/ppermute | solution.py:422
  32.5 21.7 %collective-permute-start.1 = (f32[4,128,128]{2,1,0:T(8,128)}, f32[4,128,128]{2,1,0:T(8,128)}, u32[]{:S(2)}, u32[]{:S(2)}) collective-permute-start(f32[4,128,128]{2,1,0:T(8,128)} %get-tuple-element.24), channel_id=1, source_target_pairs={{0,3},{1,0},{2,1},{3,2},{4,7},{5,4},{6,5},{7,6},{8,11},{9,8},{10,9... | collective-permute-start | bytes 786440 | tf_op jit(solution)/shard_map/ppermute | solution.py:422
  34.7 19.5 %collective-permute-start.2 = (f32[4,128,128]{2,1,0:T(8,128)}, f32[4,128,128]{2,1,0:T(8,128)}, u32[]{:S(2)}, u32[]{:S(2)}) collective-permute-start(f32[4,128,128]{2,1,0:T(8,128)} %get-tuple-element.25), channel_id=1, source_target_pairs={{0,2},{1,3},{2,0},{3,1},{4,6},{5,7},{6,4},{7,5},{8,10},{9,11},{10,... | collective-permute-start | bytes 786440 | tf_op jit(solution)/shard_map/ppermute | solution.py:422
  34.7 12.5 %collective-permute-start.10 = (f32[136,128]{1,0:T(8,128)S(1)}, f32[136,128]{1,0:T(8,128)S(1)}, u32[]{:S(2)}, u32[]{:S(2)}) collective-permute-start(f32[136,128]{1,0:T(8,128)S(1)} %get-tuple-element.43), channel_id=1, source_target_pairs={{0,3},{1,0},{2,1},{3,2},{4,7},{5,4},{6,5},{7,6},{8,11},{9,8},{10,9... | collective-permute-start | bytes 208904 | tf_op jit(solution)/shard_map/ppermute | solution.py:422
  37.2 10.0 %collective-permute-start.9 = (f32[136,128]{1,0:T(8,128)S(1)}, f32[136,128]{1,0:T(8,128)S(1)}, u32[]{:S(2)}, u32[]{:S(2)}) collective-permute-start(f32[136,128]{1,0:T(8,128)S(1)} %get-tuple-element.44), channel_id=1, source_target_pairs={{0,1},{1,2},{2,3},{3,0},{4,5},{5,6},{6,7},{7,4},{8,9},{9,10},{10,1... | collective-permute-start | bytes 208904 | tf_op jit(solution)/shard_map/ppermute | solution.py:422
  48.5 34.2 %all-to-all-start = ((f32[16,128,128]{2,1,0:T(8,128)}), f32[16,128,128]{2,1,0:T(8,128)S(1)}, u32[]{:S(2)}, u32[]{:S(2)}) async-start(f32[16,128,128]{2,1,0:T(8,128)} %get-tuple-element.39), calls=%async_computation | async-start | bytes 2097152 | tf_op jit(solution)/shard_map/all_to_all | solution.py:453
  54.2 14.7 %copy-start.4 = (f32[128]{0:T(128)S(1)}, f32[128]{0:T(128)}, u32[]{:S(2)}) copy-start(f32[128]{0:T(128)} %param.21) | copy-start | bytes 1540
  56.1 12.8 %copy-start.2 = (f32[32,4]{1,0:T(8,128)S(1)}, f32[32,4]{1,0:T(8,128)}, u32[]{:S(2)}) copy-start(f32[32,4]{1,0:T(8,128)} %copy-done.1) | copy-start | bytes 1540
  56.1 12.2 %collective-permute-start.5 = (f32[128,128]{1,0:T(8,128)}, f32[128,128]{1,0:T(8,128)S(1)}, u32[]{:S(2)}, u32[]{:S(2)}) collective-permute-start(f32[128,128]{1,0:T(8,128)} %get-tuple-element.46), channel_id=1, source_target_pairs={{0,8},{1,9},{2,10},{3,11},{4,12},{5,13},{6,14},{7,15},{8,0},{9,1},... | collective-permute-start | bytes 196616 | tf_op jit(solution)/shard_map/ppermute | solution.py:419
  59.6 8.8 %collective-permute-start.4 = (f32[128,128]{1,0:T(8,128)}, f32[128,128]{1,0:T(8,128)S(1)}, u32[]{:S(2)}, u32[]{:S(2)}) collective-permute-start(f32[128,128]{1,0:T(8,128)} %get-tuple-element.47), channel_id=1, source_target_pairs={{0,12},{1,13},{2,14},{3,15},{4,0},{5,1},{6,2},{7,3},{8,4},{9,5},{1... | collective-permute-start | bytes 196616 | tf_op jit(solution)/shard_map/ppermute | solution.py:419
  60.7 8.2 %collective-permute-start.3 = (f32[128,128]{1,0:T(8,128)}, f32[128,128]{1,0:T(8,128)S(1)}, u32[]{:S(2)}, u32[]{:S(2)}) collective-permute-start(f32[128,128]{1,0:T(8,128)} %get-tuple-element.48), channel_id=1, source_target_pairs={{0,4},{1,5},{2,6},{3,7},{4,8},{5,9},{6,10},{7,11},{8,12},{9,13},{1... | collective-permute-start | bytes 196616 | tf_op jit(solution)/shard_map/ppermute | solution.py:419
  68.9 0.8 copy-start.3
  72.2 1.4 %collective-permute-start.12 = (f32[4,32,256]{2,1,0:T(8,128)S(1)}, f32[4,32,256]{2,1,0:T(8,128)S(1)}, u32[]{:S(2)}, u32[]{:S(2)}) collective-permute-start(f32[4,32,256]{2,1,0:T(8,128)S(1)} %get-tuple-element.34), channel_id=1, source_target_pairs={{0,16},{16,0},{32,48},{48,32},{64,80},{80,64},{96,112},{112,96},{1... | collective-permute-start | bytes 393224 | tf_op jit(solution)/shard_map/ppermute | solution.py:333
  73.6 5.9 %collective-permute-start.13 = (f32[32,256]{1,0:T(8,128)S(1)}, f32[32,256]{1,0:T(8,128)S(1)}, u32[]{:S(2)}, u32[]{:S(2)}) collective-permute-start(f32[32,256]{1,0:T(8,128)S(1)} %get-tuple-element.36), channel_id=1, source_target_pairs={{0,32},{16,48},{32,64},{48,80},{64,96},{80,112},{96,0},{112,16},{1... | collective-permute-start | bytes 98312 | tf_op jit(solution)/shard_map/ppermute | solution.py:343
  75.3 5.4 %collective-permute-start.14 = (f32[32,256]{1,0:T(8,128)S(1)}, f32[32,256]{1,0:T(8,128)S(1)}, u32[]{:S(2)}, u32[]{:S(2)}) collective-permute-start(f32[32,256]{1,0:T(8,128)S(1)} %get-tuple-element.37), channel_id=1, source_target_pairs={{0,64},{16,80},{32,96},{48,112},{64,0},{80,16},{96,32},{112,48},{1... | collective-permute-start | bytes 98312 | tf_op jit(solution)/shard_map/ppermute | solution.py:343
  78.2 3.9 %collective-permute-start.15 = (f32[32,256]{1,0:T(8,128)S(1)}, f32[32,256]{1,0:T(8,128)S(1)}, u32[]{:S(2)}, u32[]{:S(2)}) collective-permute-start(f32[32,256]{1,0:T(8,128)S(1)} %get-tuple-element.38), channel_id=1, source_target_pairs={{0,96},{16,112},{32,0},{48,16},{64,32},{80,48},{96,64},{112,80},{1... | collective-permute-start | bytes 98312 | tf_op jit(solution)/shard_map/ppermute | solution.py:343
where the time goes:
time: 91.3 us; the launch traced here: 90.8 us
  starting transfers between devices  32 us (35%)
  waiting for transfers between devices  28.6 us (31%)
  Pallas kernels  21.9 us (24%)
  matrix products  4.13 us (5%)
  other arithmetic  2.55 us (3%)
    ppermute x6, waiting for transfers between devices, along_x(): lax.ppermute(value, 'row', [(n, (n + SIDE * step) % parts) for n in range...  16.1 us
    ppermute x6, starting transfers between devices, along_x(): lax.ppermute(value, 'row', [(n, (n + SIDE * step) % parts) for n in range...  10.7 us
    pallas_call x1, Pallas kernels, decode(): pl.pallas_call(read_kernel, in_specs=[any_space] * 8, out_specs=[in_vmem]...  10.1 us
    ppermute x6, starting transfers between devices, along_z(): lax.ppermute(value, 'row', [(n, n // SIDE * SIDE + (n + step) % SIDE) for...  9.66 us
    ppermute x6, waiting for transfers between devices, along_z(): lax.ppermute(value, 'row', [(n, n // SIDE * SIDE + (n + step) % SIDE) for...  8.67 us
    pallas_call x1, Pallas kernels, decode(): pl.pallas_call(update_kernel, in_specs=[in_vmem, any_space, any_space, an...  8.12 us
    ppermute x3, starting transfers between devices, head_exchange(): lax.ppermute(part, 'head', [(h, (h + 2 * s) % heads) for h in range(heads)])  5.89 us
    all_to_all x1, starting transfers between devices, decode(): delta = lax.all_to_all(delta_sent, 'row', 0, 0, tiled=True)  5.68 us
  transfers between devices with their start and end apart: 17, of which 9 were waited for; matrix products, arithmetic and copies ran while one was open for 7% of the time, Pallas kernels for 4%

commit v1 on v0

--- a/solution.py
+++ b/solution.py
@@ -36,8 +36,8 @@
     by_x, by_z = rest[0:SIDE], rest[SIDE : 2 * SIDE]
     keys_hbm, decay_hbm, decay_own, beta_own = rest[2 * SIDE : 2 * SIDE + 4]
     hidden, weights, w_decay, w_beta, decay_log, dt_bias, state = rest[2 * SIDE + 4 : 2 * SIDE + 11]
-    reads_k, left, picks, sums, keys_all, decay_all, beta_all = rest[2 * SIDE + 11 : 2 * SIDE + 18]
-    in_sems, hidden_sems, state_sems, k_sems, out_sems = rest[2 * SIDE + 18 :]
+    reads_k, reads_q, left, picks, sums, keys_all, decay_all, beta_all = rest[2 * SIDE + 11 : 2 * SIDE + 19]
+    in_sems, hidden_sems, state_sems, k_sems, q_sems, out_sems = rest[2 * SIDE + 19 :]
     me = lax.axis_index("row")
     my_x, my_z = me // SIDE, me % SIDE
     _, rows, heads = state.shape[0:3]
@@ -74,6 +74,9 @@
 
     def k_copy(s, to):
         return pltpu.make_async_copy(reads_k.at[s], to, k_sems.at[s])
+
+    def q_copy(s, t):
+        return pltpu.make_async_copy(reads_q.at[t, s], by_z[t].at[s], q_sems.at[t, s])
 
     ahead = 2
     for n in range(ahead):
@@ -142,8 +145,10 @@
                         to = (g * group + j) * rows + first
                         lanes = slice(j * LANES, (j + 1) * LANES)
                         reads_k[s, t, to : to + few] = read[few:, lanes]
-                        by_z[t][s, to : to + few] = read[0:few, lanes]
+                        reads_q[t, s, to : to + few] = read[0:few, lanes]
             reads_k[s, t, heads * rows :] = pltpu.roll(sums[...], (LANES - p * rows) % LANES, 1)
+        for t in range(SIDE):
+            q_copy(s, t).start()
         for k in range(SIDE):
 
             @pl.when(s == k)
@@ -162,6 +167,8 @@
     beta_own[...] = beta_all[mine]
     for k in range(SIDE):
         k_copy(k, by_x[k]).wait()
+        for t in range(SIDE):
+            q_copy(k, t).wait()
     for copy in outputs:
         copy.wait()
 
@@ -376,9 +383,9 @@
     *sent, keys, decay_all, decay, beta = pl.pallas_call(
         read_kernel,
         in_specs=[any_space] * 8,
-        out_specs=[in_vmem] * (2 * SIDE) + [any_space] * 2 + [in_vmem] * 2,
-        out_shape=[pltpu.VMEM(per_k, f32)] * SIDE
-        + [pltpu.VMEM(per_q, f32)] * SIDE
+        out_specs=[any_space] * (2 * SIDE + 2) + [in_vmem] * 2,
+        out_shape=[pltpu.HBM(per_k, f32)] * SIDE
+        + [pltpu.HBM(per_q, f32)] * SIDE
         + [pltpu.HBM((key_rows, seqs), f32), pltpu.HBM((seqs, heads), f32)]
         + [jax.ShapeDtypeStruct((rows, heads), f32)] * 2,
         scratch_shapes=[
@@ -390,6 +397,7 @@
             pltpu.VMEM((1, heads), f32),
             pltpu.VMEM((parts, rows, heads, SUB, LANES), f32),
             pltpu.VMEM((SIDE, *per_k), f32),
+            pltpu.VMEM((SIDE, *per_q), f32),
             pltpu.VMEM((2 * key_rows // SUB, 2 * LANES // BLOCK, BLOCK, BLOCK * SUB), jnp.bfloat16),
             pltpu.VMEM((2 * key_rows // SUB, LANES, BLOCK * SUB), jnp.bfloat16),
             pltpu.VMEM((SUB, LANES), f32),
@@ -400,6 +408,7 @@
             pltpu.SemaphoreType.DMA((seqs // LANES,)),
             pltpu.SemaphoreType.DMA((parts,)),
             pltpu.SemaphoreType.DMA((SIDE,)),
+            pltpu.SemaphoreType.DMA((SIDE, SIDE)),
             pltpu.SemaphoreType.DMA((2,)),
         ],
         compiler_params=limit,

time: 91.3 us -> 91.8 us (level)
  other arithmetic: 2.55 us -> 3.6 us
    add x2, other arithmetic: 1.93 us -> 2.99 us  [decode(): own[n] + got[0][n] + (got[1][n] + got[2][n])]
where the time goes in v1:
time: 91.8 us; the launch traced here: 91.3 us
  starting transfers between devices  32 us (35%)
  waiting for transfers between devices  28.2 us (31%)
  Pallas kernels  21.1 us (23%)
  matrix products  4.13 us (4%)
  other arithmetic  3.6 us (4%)
  local copies, waits for them, and re-layouts  1.53 us (2%)
    ppermute x6, waiting for transfers between devices, along_x(): lax.ppermute(value, 'row', [(n, (n + SIDE * step) % parts) for n in range...  15.6 us
    ppermute x6, starting transfers between devices, along_x(): lax.ppermute(value, 'row', [(n, (n + SIDE * step) % parts) for n in range...  10.7 us
    ppermute x6, starting transfers between devices, along_z(): lax.ppermute(value, 'row', [(n, n // SIDE * SIDE + (n + step) % SIDE) for...  9.66 us
    pallas_call x1, Pallas kernels, decode(): pl.pallas_call(read_kernel, in_specs=[any_space] * 8, out_specs=[any_spac...  9.31 us
    ppermute x6, waiting for transfers between devices, along_z(): lax.ppermute(value, 'row', [(n, n // SIDE * SIDE + (n + step) % SIDE) for...  8.68 us
    pallas_call x1, Pallas kernels, decode(): pl.pallas_call(update_kernel, in_specs=[in_vmem, any_space, any_space, an...  8.11 us
    ppermute x3, starting transfers between devices, head_exchange(): lax.ppermute(part, 'head', [(h, (h + 2 * s) % heads) for h in range(heads)])  5.89 us
    all_to_all x1, starting transfers between devices, decode(): delta = lax.all_to_all(delta_sent, 'row', 0, 0, tiled=True)  5.69 us
  transfers between devices with their start and end apart: 17, of which 9 were waited for; matrix products, arithmetic and copies ran while one was open for 7% of the time, Pallas kernels for 4%

profile of v1, /device:TPU:0, one launch (start us, length us, event | category | flops | bytes accessed | tf_op | source)
XLA Modules:
  0.0 91.3 jit_solution(18444929266595689706)
XLA Ops:
  0.6 0.0 copy-start
  0.6 9.3 %read_state.1 = (f32[4,136,128]{2,1,0:T(8,128)}, f32[4,136,128]{2,1,0:T(8,128)}, f32[4,136,128]{2,1,0:T(8,128)}, f32[4,136,128]{2,1,0:T(8,128)}, f32[4,128,128]{...) custom-call(bf16[512,2048]{1,0:T(8,128)(2,1)} %hidden_hbm.1, ...), custom_call_target="tpu_custom_call" | custom-call | tf_op jit(solution)/shard_map/read_state/pallas_call | solution.py:383
  10.0 1.7 %collective-permute-start.6 = (f32[4,136,128]{2,1,0:T(8,128)}, f32[4,136,128]{2,1,0:T(8,128)S(1)}, u32[]{:S(2)}, u32[]{:S(2)}) collective-permute-start(f32[4,136,128]{2,1,0:T(8,128)} %get-tuple-element.27), channel_id=1, source_target_pairs={{0,4},{1,5},{2,6},{3,7},{4,8},{5,9},{6,10},{7,11},{8,12},{9,13},{1... | collective-permute-start | bytes 835592 | tf_op jit(solution)/shard_map/ppermute | solution.py:428
  11.6 1.6 %collective-permute-start.7 = (f32[4,136,128]{2,1,0:T(8,128)}, f32[4,136,128]{2,1,0:T(8,128)S(1)}, u32[]{:S(2)}, u32[]{:S(2)}) collective-permute-start(f32[4,136,128]{2,1,0:T(8,128)} %get-tuple-element.28), channel_id=1, source_target_pairs={{0,12},{1,13},{2,14},{3,15},{4,0},{5,1},{6,2},{7,3},{8,4},{9,5},{1... | collective-permute-start | bytes 835592 | tf_op jit(solution)/shard_map/ppermute | solution.py:428
  13.3 1.9 %collective-permute-start.8 = (f32[4,136,128]{2,1,0:T(8,128)}, f32[4,136,128]{2,1,0:T(8,128)S(1)}, u32[]{:S(2)}, u32[]{:S(2)}) collective-permute-start(f32[4,136,128]{2,1,0:T(8,128)} %get-tuple-element.29), channel_id=1, source_target_pairs={{0,8},{1,9},{2,10},{3,11},{4,12},{5,13},{6,14},{7,15},{8,0},{9,1},... | collective-permute-start | bytes 835592 | tf_op jit(solution)/shard_map/ppermute | solution.py:428
  15.2 4.6 %collective-permute-done.6 = f32[4,136,128]{2,1,0:T(8,128)S(1)} collective-permute-done((f32[4,136,128]{2,1,0:T(8,128)}, f32[4,136,128]{2,1,0:T(8,128)S(1)}, u32[]{:S(2)}, u32[]{:S(2)}) %collective-permute-start.6) | collective-permute-done | bytes 278560 | tf_op jit(solution)/shard_map/ppermute | solution.py:428
  19.8 1.6 %collective-permute-done.7 = f32[4,136,128]{2,1,0:T(8,128)S(1)} collective-permute-done((f32[4,136,128]{2,1,0:T(8,128)}, f32[4,136,128]{2,1,0:T(8,128)S(1)}, u32[]{:S(2)}, u32[]{:S(2)}) %collective-permute-start.7) | collective-permute-done | bytes 278560 | tf_op jit(solution)/shard_map/ppermute | solution.py:428
  21.4 5.5 %collective-permute-done.8 = f32[4,136,128]{2,1,0:T(8,128)S(1)} collective-permute-done((f32[4,136,128]{2,1,0:T(8,128)}, f32[4,136,128]{2,1,0:T(8,128)S(1)}, u32[]{:S(2)}, u32[]{:S(2)}) %collective-permute-start.8) | collective-permute-done | bytes 278560 | tf_op jit(solution)/shard_map/ppermute | solution.py:428
  26.9 1.1 %fusion.15 = (f32[136,128]{1,0:T(8,128)S(1)}, f32[136,128]{1,0:T(8,128)S(1)}, f32[136,128]{1,0:T(8,128)S(1)}, f32[136,128]{1,0:T(8,128)S(1)}) fusion(f32[4,136,128]{2,1,0:T(8,128)S(1)} %collective-permute-done.8, f32[4,136,128]{2,1,0:T(8,128)S(1)} %collective-permute-done.7, f32[4,136,128]{2,1,0:T(8,128)S(1)} %collective-permute-done.6, ...), kind=kLoop, calls=%fused_computation.12 | loop fusion | flops 208896 | bytes 1392640 | tf_op jit(solution)/shard_map/add | solution.py:437
  28.0 4.0 %collective-permute-start.11 = (f32[136,128]{1,0:T(8,128)S(1)}, f32[136,128]{1,0:T(8,128)S(1)}, u32[]{:S(2)}, u32[]{:S(2)}) collective-permute-start(f32[136,128]{1,0:T(8,128)S(1)} %get-tuple-element.42), channel_id=1, source_target_pairs={{0,2},{1,3},{2,0},{3,1},{4,6},{5,7},{6,4},{7,5},{8,10},{9,11},{10,... | collective-permute-start | bytes 208904 | tf_op jit(solution)/shard_map/ppermute | solution.py:431
  31.9 1.0 %collective-permute-start = (f32[4,128,128]{2,1,0:T(8,128)}, f32[4,128,128]{2,1,0:T(8,128)S(1)}, u32[]{:S(2)}, u32[]{:S(2)}) collective-permute-start(f32[4,128,128]{2,1,0:T(8,128)} %get-tuple-element.23), channel_id=1, source_target_pairs={{0,1},{1,2},{2,3},{3,0},{4,5},{5,6},{6,7},{7,4},{8,9},{9,10},{10,1... | collective-permute-start | bytes 786440 | tf_op jit(solution)/shard_map/ppermute | solution.py:431
  32.9 2.2 %collective-permute-start.1 = (f32[4,128,128]{2,1,0:T(8,128)}, f32[4,128,128]{2,1,0:T(8,128)}, u32[]{:S(2)}, u32[]{:S(2)}) collective-permute-start(f32[4,128,128]{2,1,0:T(8,128)} %get-tuple-element.24), channel_id=1, source_target_pairs={{0,3},{1,0},{2,1},{3,2},{4,7},{5,4},{6,5},{7,6},{8,11},{9,8},{10,9... | collective-permute-start | bytes 786440 | tf_op jit(solution)/shard_map/ppermute | solution.py:431
  35.2 0.0 collective-permute-start.2
  35.2 2.5 %collective-permute-start.10 = (f32[136,128]{1,0:T(8,128)S(1)}, f32[136,128]{1,0:T(8,128)S(1)}, u32[]{:S(2)}, u32[]{:S(2)}) collective-permute-start(f32[136,128]{1,0:T(8,128)S(1)} %get-tuple-element.43), channel_id=1, source_target_pairs={{0,3},{1,0},{2,1},{3,2},{4,7},{5,4},{6,5},{7,6},{8,11},{9,8},{10,9... | collective-permute-start | bytes 208904 | tf_op jit(solution)/shard_map/ppermute | solution.py:431
  37.6 0.0 collective-permute-done.11.refs_3_
  37.6 0.0 collective-permute-start.9
  37.6 0.0 copy-done
  37.6 1.4 %fusion.4.refs_4_ = f32[4,32,128]{2,1,0:T(8,128)S(1)} fusion(bf16[2048,4,128]{2,1,0:T(4,128)(2,1)S(1)} %copy-done, bf16[512,2048]{1,0:T(8,128)(2,1)} %hidden_hbm.1, s32[]{:T(128)S(6)} %select_n.16), kind=kOutput, calls=%fused_computation.4 | convolution fusion | flops 67108864 | bytes 2293764 | tf_op jit(solution)/shard_map/bd,dhv->hbv/dot_general | solution.py:444
  39.0 8.7 %collective-permute-done.10.refs_2_ = f32[136,128]{1,0:T(8,128)S(1)} collective-permute-done((f32[136,128]{1,0:T(8,128)S(1)}, f32[136,128]{1,0:T(8,128)S(1)}, u32[]{:S(2)}, u32[]{:S(2)}) %collective-permute-start.10) | collective-permute-done | bytes 69664 | tf_op jit(solution)/shard_map/ppermute | solution.py:431
  47.7 0.0 collective-permute-done.9.refs_1_
  47.7 1.3 %owner_delta.1 = (f32[16,128,128]{2,1,0:T(8,128)}, f32[136,128]{1,0:T(8,128)S(1)}) custom-call(f32[136,128]{1,0:T(8,128)S(1)} %get-tuple-element.45.refs_0_, f32[136,128]{1,0:T(8,128)S(1)} %collective-permute-done.9.refs_1_, f32[136,128]{1,0:T(8,128)S(1)} %collective-permute-done.10.refs_2_, f32[136,128]{1,0:T(8,128)S(1)} %collective-permute-done.11.refs_3_, ...), custom_call_target="tpu_custom_call" | custom-call | tf_op jit(solution)/shard_map/owner_delta/pallas_call | solution.py:447
  49.0 5.7 %all-to-all-start = ((f32[16,128,128]{2,1,0:T(8,128)}), f32[16,128,128]{2,1,0:T(8,128)S(1)}, u32[]{:S(2)}, u32[]{:S(2)}) async-start(f32[16,128,128]{2,1,0:T(8,128)} %get-tuple-element.39), calls=%async_computation | async-start | bytes 2097152 | tf_op jit(solution)/shard_map/all_to_all | solution.py:462
  54.6 0.0 copy-start.2
  54.7 0.0 collective-permute-done
  54.7 0.0 copy-start.3
  54.7 0.0 collective-permute-done.1
  54.7 0.0 collective-permute-done.2
  54.7 0.7 copy-done.3
  55.4 1.9 %fusion.23 = (f32[128,128]{1,0:T(8,128)}, f32[128,128]{1,0:T(8,128)}, f32[128,128]{1,0:T(8,128)}, f32[128,128]{1,0:T(8,128)S(1)}) fusion(f32[4,128,128]{2,1,0:T(8,128)} %collective-permute-done.2, f32[4,128,128]{2,1,0:T(8,128)} %collective-permute-done.1, f32[4,128,128]{2,1,0:T(8,128)} %copy-done.3, f32[4,128,128]{2,1,0:T(8,128)} %get-tuple-element.22), kind=kLoop, calls=%fused_computation.28 | loop fusion | flops 196608 | bytes 1310720 | tf_op jit(solution)/shard_map/add | solution.py:437
  57.3 3.4 %collective-permute-start.5 = (f32[128,128]{1,0:T(8,128)}, f32[128,128]{1,0:T(8,128)S(1)}, u32[]{:S(2)}, u32[]{:S(2)}) collective-permute-start(f32[128,128]{1,0:T(8,128)} %get-tuple-element.46), channel_id=1, source_target_pairs={{0,8},{1,9},{2,10},{3,11},{4,12},{5,13},{6,14},{7,15},{8,0},{9,1},... | collective-permute-start | bytes 196616 | tf_op jit(solution)/shard_map/ppermute | solution.py:428
  60.7 1.2 %collective-permute-start.4 = (f32[128,128]{1,0:T(8,128)}, f32[128,128]{1,0:T(8,128)S(1)}, u32[]{:S(2)}, u32[]{:S(2)}) collective-permute-start(f32[128,128]{1,0:T(8,128)} %get-tuple-element.47), channel_id=1, source_target_pairs={{0,12},{1,13},{2,14},{3,15},{4,0},{5,1},{6,2},{7,3},{8,4},{9,5},{1... | collective-permute-start | bytes 196616 | tf_op jit(solution)/shard_map/ppermute | solution.py:428
  61.9 0.9 collective-permute-start.3
  62.8 2.8 %fusion.7.refs_5_ = f32[4,32,128]{2,1,0:T(8,128)} fusion(bf16[2048,4,128]{2,1,0:T(4,128)(2,1)} %param.16, bf16[512,2048]{1,0:T(8,128)(2,1)} %hidden_hbm.1, s32[]{:T(128)S(6)} %select_n.16), kind=kOutput, calls=%fused_computation.5 | convolution fusion | flops 67108864 | bytes 2293764 | tf_op jit(solution)/shard_map/bd,dhv->hbv/dot_general | solution.py:445
  65.5 3.3 %collective-permute-done.5.refs_3_ = f32[128,128]{1,0:T(8,128)S(1)} collective-permute-done((f32[128,128]{1,0:T(8,128)}, f32[128,128]{1,0:T(8,128)S(1)}, u32[]{:S(2)}, u32[]{:S(2)}) %collective-permute-start.5) | collective-permute-done | bytes 65568 | tf_op jit(solution)/shard_map/ppermute | solution.py:428
  68.8 0.0 collective-permute-done.4.refs_2_
  68.8 0.6 collective-permute-done.3.refs_1_
  69.4 0.0 copy-done.2
  69.4 0.0 copy-start.1
  69.4 0.8 copy-done.1
  70.2 0.3 owner_norm.1.normed
  70.6 2.1 %project_out.1 = (f32[4,32,256]{2,1,0:T(8,128)S(1)}, f32[4,32,256]{2,1,0:T(8,128)S(1)}) custom-call(s32[1]{0:T(128)} %bitcast.1.core, bf16[32,512]{1,0:T(8,128)(2,1)S(1)} %owner_norm.1.normed, bf16[512,2048]{1,0:T(8,128)(2,1)} %bitcast.40), custom_call_target="tpu_custom_call" | custom-call | tf_op jit(solution)/shard_map/project_out/pallas_call | solution.py:331
  72.6 0.1 collective-permute-start.12
  72.8 1.3 %collective-permute-done.12.got = f32[4,32,256]{2,1,0:T(8,128)S(1)} collective-permute-done((f32[4,32,256]{2,1,0:T(8,128)S(1)}, f32[4,32,256]{2,1,0:T(8,128)S(1)}, u32[]{:S(2)}, u32[]{:S(2)}) %collective-permute-start.12) | collective-permute-done | bytes 131104 | tf_op jit(solution)/shard_map/ppermute | solution.py:340
  74.1 1.6 %collective-permute-start.13 = (f32[32,256]{1,0:T(8,128)S(1)}, f32[32,256]{1,0:T(8,128)S(1)}, u32[]{:S(2)}, u32[]{:S(2)}) collective-permute-start(f32[32,256]{1,0:T(8,128)S(1)} %get-tuple-element.36), channel_id=1, source_target_pairs={{0,32},{16,48},{32,64},{48,80},{64,96},{80,112},{96,0},{112,16},{1... | collective-permute-start | bytes 98312 | tf_op jit(solution)/shard_map/ppermute | solution.py:350
  75.7 2.9 %collective-permute-start.14 = (f32[32,256]{1,0:T(8,128)S(1)}, f32[32,256]{1,0:T(8,128)S(1)}, u32[]{:S(2)}, u32[]{:S(2)}) collective-permute-start(f32[32,256]{1,0:T(8,128)S(1)} %get-tuple-element.37), channel_id=1, source_target_pairs={{0,64},{16,80},{32,96},{48,112},{64,0},{80,16},{96,32},{112,48},{1... | collective-permute-start | bytes 98312 | tf_op jit(solution)/shard_map/ppermute | solution.py:350
  78.6 1.3 %collective-permute-start.15 = (f32[32,256]{1,0:T(8,128)S(1)}, f32[32,256]{1,0:T(8,128)S(1)}, u32[]{:S(2)}, u32[]{:S(2)}) collective-permute-start(f32[32,256]{1,0:T(8,128)S(1)} %get-tuple-element.38), channel_id=1, source_target_pairs={{0,96},{16,112},{32,0},{48,16},{64,32},{80,48},{96,64},{112,80},{1... | collective-permute-start | bytes 98312 | tf_op jit(solution)/shard_map/ppermute | solution.py:350
  80.0 0.0 collective-permute-done.13
  80.0 1.2 %collective-permute-done.14 = f32[32,256]{1,0:T(8,128)S(1)} collective-permute-done((f32[32,256]{1,0:T(8,128)S(1)}, f32[32,256]{1,0:T(8,128)S(1)}, u32[]{:S(2)}, u32[]{:S(2)}) %collective-permute-start.14) | collective-permute-done | bytes 32800 | tf_op jit(solution)/shard_map/ppermute | solution.py:350
  81.2 1.4 %collective-permute-done.15 = f32[32,256]{1,0:T(8,128)S(1)} collective-permute-done((f32[32,256]{1,0:T(8,128)S(1)}, f32[32,256]{1,0:T(8,128)S(1)}, u32[]{:S(2)}, u32[]{:S(2)}) %collective-permute-start.15) | collective-permute-done | bytes 32800 | tf_op jit(solution)/shard_map/ppermute | solution.py:350
  82.6 0.6 add_convert_fusion
  83.2 0.0 all-to-all-done.delta
  83.2 8.1 %update_state.1 = f32[512,4,8,128]{3,2,1,0:T(8,128)} custom-call(f32[16,128,128]{2,1,0:T(8,128)S(1)} %all-to-all-done.delta, f32[16,512]{1,0:T(8,128)} %get-tuple-element.40.keys_hbm, f32[512,4]{1,0:T(8,128)} %get-tuple-element.41.decay_hbm, f32[512,4,8,128]{3,2,1,0:T(8,128)} %state_hbm.3), custom_call_target="tpu_custom_call" | custom-call | tf_op jit(solution)/shard_map/update_state/pallas_call | solution.py:475
  (1 shorter events, 0.0 us)
Async XLA Ops:
  0.6 37.0 %copy-start = (bf16[2048,4,128]{2,1,0:T(4,128)(2,1)S(1)}, bf16[2048,4,128]{2,1,0:T(4,128)(2,1)}, u32[]{:S(2)}) copy-start(bf16[2048,4,128]{2,1,0:T(4,128)(2,1)} %param.15) | copy-start | bytes 6291460
  10.0 9.8 %collective-permute-start.6 = (f32[4,136,128]{2,1,0:T(8,128)}, f32[4,136,128]{2,1,0:T(8,128)S(1)}, u32[]{:S(2)}, u32[]{:S(2)}) collective-permute-start(f32[4,136,128]{2,1,0:T(8,128)} %get-tuple-element.27), channel_id=1, source_target_pairs={{0,4},{1,5},{2,6},{3,7},{4,8},{5,9},{6,10},{7,11},{8,12},{9,13},{1... | collective-permute-start | bytes 835592 | tf_op jit(solution)/shard_map/ppermute | solution.py:428
  11.6 9.7 %collective-permute-start.7 = (f32[4,136,128]{2,1,0:T(8,128)}, f32[4,136,128]{2,1,0:T(8,128)S(1)}, u32[]{:S(2)}, u32[]{:S(2)}) collective-permute-start(f32[4,136,128]{2,1,0:T(8,128)} %get-tuple-element.28), channel_id=1, source_target_pairs={{0,12},{1,13},{2,14},{3,15},{4,0},{5,1},{6,2},{7,3},{8,4},{9,5},{1... | collective-permute-start | bytes 835592 | tf_op jit(solution)/shard_map/ppermute | solution.py:428
  13.3 13.6 %collective-permute-start.8 = (f32[4,136,128]{2,1,0:T(8,128)}, f32[4,136,128]{2,1,0:T(8,128)S(1)}, u32[]{:S(2)}, u32[]{:S(2)}) collective-permute-start(f32[4,136,128]{2,1,0:T(8,128)} %get-tuple-element.29), channel_id=1, source_target_pairs={{0,8},{1,9},{2,10},{3,11},{4,12},{5,13},{6,14},{7,15},{8,0},{9,1},... | collective-permute-start | bytes 835592 | tf_op jit(solution)/shard_map/ppermute | solution.py:428
  28.0 9.7 %collective-permute-start.11 = (f32[136,128]{1,0:T(8,128)S(1)}, f32[136,128]{1,0:T(8,128)S(1)}, u32[]{:S(2)}, u32[]{:S(2)}) collective-permute-start(f32[136,128]{1,0:T(8,128)S(1)} %get-tuple-element.42), channel_id=1, source_target_pairs={{0,2},{1,3},{2,0},{3,1},{4,6},{5,7},{6,4},{7,5},{8,10},{9,11},{10,... | collective-permute-start | bytes 208904 | tf_op jit(solution)/shard_map/ppermute | solution.py:431
  31.9 22.7 %collective-permute-start = (f32[4,128,128]{2,1,0:T(8,128)}, f32[4,128,128]{2,1,0:T(8,128)S(1)}, u32[]{:S(2)}, u32[]{:S(2)}) collective-permute-start(f32[4,128,128]{2,1,0:T(8,128)} %get-tuple-element.23), channel_id=1, source_target_pairs={{0,1},{1,2},{2,3},{3,0},{4,5},{5,6},{6,7},{7,4},{8,9},{9,10},{10,1... | collective-permute-start | bytes 786440 | tf_op jit(solution)/shard_map/ppermute | solution.py:431
  32.9 21.8 %collective-permute-start.1 = (f32[4,128,128]{2,1,0:T(8,128)}, f32[4,128,128]{2,1,0:T(8,128)}, u32[]{:S(2)}, u32[]{:S(2)}) collective-permute-start(f32[4,128,128]{2,1,0:T(8,128)} %get-tuple-element.24), channel_id=1, source_target_pairs={{0,3},{1,0},{2,1},{3,2},{4,7},{5,4},{6,5},{7,6},{8,11},{9,8},{10,9... | collective-permute-start | bytes 786440 | tf_op jit(solution)/shard_map/ppermute | solution.py:431
  35.2 19.5 %collective-permute-start.2 = (f32[4,128,128]{2,1,0:T(8,128)}, f32[4,128,128]{2,1,0:T(8,128)}, u32[]{:S(2)}, u32[]{:S(2)}) collective-permute-start(f32[4,128,128]{2,1,0:T(8,128)} %get-tuple-element.25), channel_id=1, source_target_pairs={{0,2},{1,3},{2,0},{3,1},{4,6},{5,7},{6,4},{7,5},{8,10},{9,11},{10,... | collective-permute-start | bytes 786440 | tf_op jit(solution)/shard_map/ppermute | solution.py:431
  35.2 12.5 %collective-permute-start.10 = (f32[136,128]{1,0:T(8,128)S(1)}, f32[136,128]{1,0:T(8,128)S(1)}, u32[]{:S(2)}, u32[]{:S(2)}) collective-permute-start(f32[136,128]{1,0:T(8,128)S(1)} %get-tuple-element.43), channel_id=1, source_target_pairs={{0,3},{1,0},{2,1},{3,2},{4,7},{5,4},{6,5},{7,6},{8,11},{9,8},{10,9... | collective-permute-start | bytes 208904 | tf_op jit(solution)/shard_map/ppermute | solution.py:431
  37.6 10.0 %collective-permute-start.9 = (f32[136,128]{1,0:T(8,128)S(1)}, f32[136,128]{1,0:T(8,128)S(1)}, u32[]{:S(2)}, u32[]{:S(2)}) collective-permute-start(f32[136,128]{1,0:T(8,128)S(1)} %get-tuple-element.44), channel_id=1, source_target_pairs={{0,1},{1,2},{2,3},{3,0},{4,5},{5,6},{6,7},{7,4},{8,9},{9,10},{10,1... | collective-permute-start | bytes 208904 | tf_op jit(solution)/shard_map/ppermute | solution.py:431
  49.0 34.2 %all-to-all-start = ((f32[16,128,128]{2,1,0:T(8,128)}), f32[16,128,128]{2,1,0:T(8,128)S(1)}, u32[]{:S(2)}, u32[]{:S(2)}) async-start(f32[16,128,128]{2,1,0:T(8,128)} %get-tuple-element.39), calls=%async_computation | async-start | bytes 2097152 | tf_op jit(solution)/shard_map/all_to_all | solution.py:462
  54.6 14.7 %copy-start.2 = (f32[128]{0:T(128)S(1)}, f32[128]{0:T(128)}, u32[]{:S(2)}) copy-start(f32[128]{0:T(128)} %param.21) | copy-start | bytes 1540
  54.7 0.7 copy-start.3
  57.3 11.5 %collective-permute-start.5 = (f32[128,128]{1,0:T(8,128)}, f32[128,128]{1,0:T(8,128)S(1)}, u32[]{:S(2)}, u32[]{:S(2)}) collective-permute-start(f32[128,128]{1,0:T(8,128)} %get-tuple-element.46), channel_id=1, source_target_pairs={{0,8},{1,9},{2,10},{3,11},{4,12},{5,13},{6,14},{7,15},{8,0},{9,1},... | collective-permute-start | bytes 196616 | tf_op jit(solution)/shard_map/ppermute | solution.py:428
  60.7 8.1 %collective-permute-start.4 = (f32[128,128]{1,0:T(8,128)}, f32[128,128]{1,0:T(8,128)S(1)}, u32[]{:S(2)}, u32[]{:S(2)}) collective-permute-start(f32[128,128]{1,0:T(8,128)} %get-tuple-element.47), channel_id=1, source_target_pairs={{0,12},{1,13},{2,14},{3,15},{4,0},{5,1},{6,2},{7,3},{8,4},{9,5},{1... | collective-permute-start | bytes 196616 | tf_op jit(solution)/shard_map/ppermute | solution.py:428
  61.9 7.5 %collective-permute-start.3 = (f32[128,128]{1,0:T(8,128)}, f32[128,128]{1,0:T(8,128)S(1)}, u32[]{:S(2)}, u32[]{:S(2)}) collective-permute-start(f32[128,128]{1,0:T(8,128)} %get-tuple-element.48), channel_id=1, source_target_pairs={{0,4},{1,5},{2,6},{3,7},{4,8},{5,9},{6,10},{7,11},{8,12},{9,13},{1... | collective-permute-start | bytes 196616 | tf_op jit(solution)/shard_map/ppermute | solution.py:428
  69.4 0.8 copy-start.1
  72.6 1.4 %collective-permute-start.12 = (f32[4,32,256]{2,1,0:T(8,128)S(1)}, f32[4,32,256]{2,1,0:T(8,128)S(1)}, u32[]{:S(2)}, u32[]{:S(2)}) collective-permute-start(f32[4,32,256]{2,1,0:T(8,128)S(1)} %get-tuple-element.34), channel_id=1, source_target_pairs={{0,16},{16,0},{32,48},{48,32},{64,80},{80,64},{96,112},{112,96},{1... | collective-permute-start | bytes 393224 | tf_op jit(solution)/shard_map/ppermute | solution.py:340
  74.1 5.9 %collective-permute-start.13 = (f32[32,256]{1,0:T(8,128)S(1)}, f32[32,256]{1,0:T(8,128)S(1)}, u32[]{:S(2)}, u32[]{:S(2)}) collective-permute-start(f32[32,256]{1,0:T(8,128)S(1)} %get-tuple-element.36), channel_id=1, source_target_pairs={{0,32},{16,48},{32,64},{48,80},{64,96},{80,112},{96,0},{112,16},{1... | collective-permute-start | bytes 98312 | tf_op jit(solution)/shard_map/ppermute | solution.py:350
  75.7 5.4 %collective-permute-start.14 = (f32[32,256]{1,0:T(8,128)S(1)}, f32[32,256]{1,0:T(8,128)S(1)}, u32[]{:S(2)}, u32[]{:S(2)}) collective-permute-start(f32[32,256]{1,0:T(8,128)S(1)} %get-tuple-element.37), channel_id=1, source_target_pairs={{0,64},{16,80},{32,96},{48,112},{64,0},{80,16},{96,32},{112,48},{1... | collective-permute-start | bytes 98312 | tf_op jit(solution)/shard_map/ppermute | solution.py:350
  78.6 3.9 %collective-permute-start.15 = (f32[32,256]{1,0:T(8,128)S(1)}, f32[32,256]{1,0:T(8,128)S(1)}, u32[]{:S(2)}, u32[]{:S(2)}) collective-permute-start(f32[32,256]{1,0:T(8,128)S(1)} %get-tuple-element.38), channel_id=1, source_target_pairs={{0,96},{16,112},{32,0},{48,16},{64,32},{80,48},{96,64},{112,80},{1... | collective-permute-start | bytes 98312 | tf_op jit(solution)/shard_map/ppermute | solution.py:350
